TPU v7x, 512 devices: a whole 4x8x8 slice. The times are simulated.
512 devices in a mesh: row: 16 (over z, core), col: 4 (over x), depth: 8 (over y).
Axes of the slice: x: 4, y: 8, z: 8, core: 2. Of those that a mesh axis runs over, the one named last changes fastest.
Arguments:
- intersection_re: bfloat16 [8, 4096, 4096], P('depth', ('row', 'col')), may hold values from -1 to 1, as said below
- intersection_im: bfloat16 [8, 4096, 4096], P('depth', ('row', 'col')), may hold values from -1 to 1, as said below
- weights: float32 [8], replicated, may hold values from 0.5 to 2
- shells: int32 [8, 3], replicated, may hold values from -2 to 2
- rotation: bfloat16 [4096, 4096], P(('row', 'col')), may hold values from -6 to 6
Outputs:
- updated: float32 [4096, 4096], P(('row', 'col'), 'depth')
Inputs may be any that keep to these rules, and one draw needn't show every extreme that they name: `intersection_re`: diagonal entries lie in 0.5 to 1. `intersection_im`: diagonal entries lie in -0.6 to 0.6.
All inputs are finite; a program needn't handle non-finite values.
Results may differ from a plain program's by a relative error of at most 0.035.
Values may be sent and summed in bfloat16 or wider, within the bound.
No kernel may reach another device: no remote copies, remote signals or barrier semaphores. Data moves between devices by JAX's collectives and lax.ppermute only.
A program may use at most 64 MiB of HBM per device.

v0:
```python
import math

import jax
import jax.numpy as jnp
from jax import lax
from jax.sharding import PartitionSpec as P

TERMS = 8


LATTICE = 0.25


def from_everyone(shard, axis):
    copies = jnp.broadcast_to(shard, (lax.axis_size(axis), *shard.shape))
    return lax.all_to_all(copies, axis, split_axis=0, concat_axis=0, tiled=True)


def in_order(parts, dim):
    dims = list(parts.shape[1:])
    dims[dim] *= parts.shape[0]
    return jnp.moveaxis(parts, 0, dim).reshape(dims)


def gather_directly(shard, axis, dim):
    parts = from_everyone(shard, axis)
    return in_order(parts, dim)


def over_copies(shard, axis):
    everything = from_everyone(shard, axis)
    return jnp.sum(everything, axis=0)


def cut_along(shard, dim, devices):
    before, after = (shard.shape[:dim], shard.shape[dim + 1 :])
    return jnp.moveaxis(shard.reshape(*before, devices, -1, *after), dim, 0)


def sum_at_owner(shard, axis, dim):
    parts = cut_along(shard, dim, lax.axis_size(axis))
    arrived = lax.all_to_all(parts, axis, split_axis=0, concat_axis=0, tiled=True)
    return arrived.sum(axis=0)


def per_device(intersection_re, intersection_im, weights, shells, rotation):
    shells_here = intersection_re.shape[0]
    slab_rows = intersection_re.shape[1]
    width = intersection_re.shape[2]
    position = lax.axis_index(("row", "col"))
    layer_index = lax.axis_index("depth")
    depth_count = lax.axis_size("depth")
    block_re = lax.dynamic_slice_in_dim(intersection_re, position * slab_rows, slab_rows, 2)
    block_im = lax.dynamic_slice_in_dim(intersection_im, position * slab_rows, slab_rows, 2)
    diag_piece = jnp.stack(
        [jnp.diagonal(block_re, axis1=1, axis2=2), jnp.diagonal(block_im, axis1=1, axis2=2)], 1
    )
    first_shell = layer_index * shells_here
    own_weights = lax.dynamic_slice_in_dim(weights, first_shell, shells_here, 0)
    own_vectors = (
        lax.dynamic_slice_in_dim(shells, first_shell, shells_here, 0).astype(jnp.float32) * LATTICE
    )
    diagonals = gather_directly(diag_piece, ("row", "col"), 2).astype(jnp.float32)
    diag_re = diagonals[:, 0]
    diag_im = diagonals[:, 1]
    phase_own = jnp.arctan2(diag_im, diag_re)
    partial_centre = -jnp.einsum("bk,bn->kn", own_weights[:, None] * own_vectors, phase_own)
    centre = over_copies(partial_centre, "depth")
    spread = phase_own + jnp.einsum("bk,kn->bn", own_vectors, centre)
    modulus = diag_re * diag_re + diag_im * diag_im
    values_re = intersection_re.astype(jnp.float32)
    values_im = intersection_im.astype(jnp.float32)
    terms = values_re * diag_re[:, None, :] + values_im * diag_im[:, None, :]
    terms = (
        terms
        - spread[:, None, :]
        * (values_im * diag_re[:, None, :] - values_re * diag_im[:, None, :])
        / modulus[:, None, :]
    )
    local_sum = jnp.sum(own_weights[:, None, None] * terms, 0)
    factor = 1.25 / math.sqrt(depth_count * shells_here)
    slab_cols = width // depth_count
    mirrored = lax.all_to_all(local_sum, ("row", "col"), split_axis=1, concat_axis=0, tiled=True).T
    operator_rows = sum_at_owner(local_sum - mirrored, "depth", 1) * factor
    operator_piece = operator_rows.astype(jnp.bfloat16)
    operator_cols = lax.all_gather(operator_piece, ("row", "col"), axis=0, tiled=True)
    accum = lax.dynamic_slice_in_dim(rotation, layer_index * slab_cols, slab_cols, 1).astype(
        jnp.float32
    )
    product = jnp.dot(rotation, operator_cols, preferred_element_type=jnp.float32)
    for order in range(1, TERMS):
        series_term = (product / order).astype(jnp.bfloat16)
        accum = accum + series_term.astype(jnp.float32)
        if order + 1 < TERMS:
            piece = gather_directly(series_term, "depth", 1)
            matching = lax.slice_in_dim(operator_cols, 0, piece.shape[1], axis=0)
            product = jnp.zeros_like(accum) + jnp.dot(
                piece, matching, preferred_element_type=jnp.float32
            )
    return accum


def solution(mesh):
    in_specs = (
        P("depth", ("row", "col"), None),
        P("depth", ("row", "col"), None),
        P(),
        P(),
        P(("row", "col"), None),
    )
    out_specs = P(("row", "col"), "depth")
    return jax.shard_map(
        per_device, mesh=mesh, in_specs=in_specs, out_specs=out_specs, check_vma=False
    )
```

profile of v0, /device:TPU:8, one launch (start us, length us, event | category | flops | bytes accessed | tf_op | source)
XLA Modules:
  0.0 354.2 jit_solution(16714782614347129712)
XLA Ops:
  6.6 0.9 dynamic-slice_bitcast_fusion
  7.5 0.9 gather_fusion.1
  8.3 0.9 gather_fusion
  9.2 0.6 broadcast_in_dim.34
  9.9 13.8 %all-to-all-start = ((bf16[64,1,2,64]{3,2,1,0:T(2,128)(2,1)}), bf16[64,1,2,64]{3,2,1,0:T(2,128)(2,1)S(1)}, u32[]{:S(2)}, u32[]{:S(2)}) async-start(bf16[64,1,2,64]{3,2,1,0:T(2,128)(2,1)} %broadcast_in_dim.34), calls=%async_computation | async-start | bytes 65536 | tf_op jit(solution)/shard_map/all_to_all | solution.py:16
  23.7 0.0 all-gather.2.cloned.1.call-start
  23.7 1.3 dynamic_slice.16
  25.7 0.9 multiply_reduce_fusion.1
  26.6 6.6 %all-to-all-done = bf16[64,1,2,64]{3,2,1,0:T(2,128)(2,1)S(1)} async-done(((bf16[64,1,2,64]{3,2,1,0:T(2,128)(2,1)}), bf16[64,1,2,64]{3,2,1,0:T(2,128)(2,1)S(1)}, u32[]{:S(2)}, u32[]{:S(2)}) %all-to-all-start) | async-done | bytes 16416 | tf_op jit(solution)/shard_map/all_to_all | solution.py:16
  33.3 0.1 reshape.91
  33.4 0.2 fusion.17
  33.7 0.1 multiply_negate_fusion
  33.7 0.1 broadcast_in_dim.35
  33.8 23.1 %all_to_all.64 = f32[8,3,4096]{2,1,0:T(4,128)S(1)} all-to-all(f32[8,3,4096]{2,1,0:T(4,128)S(1)} %broadcast_in_dim.35), channel_id=1, replica_groups=mesh['row'=16,'col'=4,'depth'=8] {'depth'}, dimensions={0} | all-to-all | bytes 786432 | tf_op jit(solution)/shard_map/all_to_all | solution.py:16
  56.9 0.1 reduce_sum.24
  57.0 0.1 fusion.15
  57.2 1.1 fusion.11
  58.3 2.2 all_to_all.43
  60.5 2.8 copy.56
  63.3 2.3 reshape.115
  65.6 33.6 %all_to_all.65 = f32[64,1,4096]{2,1,0:T(1,128)S(1)} all-to-all(f32[64,1,4096]{2,1,0:T(1,128)} %reshape.115), channel_id=1, replica_groups=mesh['row'=16,'col'=4,'depth'=8] {'row','col'}, dimensions={0} | all-to-all | bytes 2097152 | tf_op jit(solution)/shard_map/all_to_all | solution.py:83
  99.2 0.5 broadcast.60
  99.7 4.5 %reduce.4 = f32[64,4096]{1,0:T(8,128)} reduce(f32[64,1,4096]{2,1,0:T(1,128)S(1)} %all_to_all.65, f32[]{:T(128)} %broadcast.60), dimensions={1}, to_apply=%all_to_all.44.reduce_sub_computation | reduce | bytes 2097156 | tf_op jit(solution)/shard_map/all_to_all | solution.py:83
  104.2 2.0 reshape.116
  106.2 1.6 copy.39
  107.8 1.3 bitcast_subtract_fusion
  109.1 0.6 copy.54
  109.7 0.6 copy.40
  110.4 30.6 %all_to_all.66 = f32[8,64,512]{2,1,0:T(8,128)S(1)} all-to-all(f32[8,64,512]{2,1,0:T(8,128)S(1)} %copy.40), channel_id=1, replica_groups=mesh['row'=16,'col'=4,'depth'=8] {'depth'}, dimensions={0} | all-to-all | bytes 2097152 | tf_op jit(solution)/shard_map/all_to_all | solution.py:42
  140.9 0.1 reduce_sum.26
  141.0 0.6 multiply_convert_fusion
  141.7 0.0 all-gather.2.cloned.1.call-update
  141.7 78.4 %all-gather.2.cloned.1.call-done = bf16[4096,512]{1,0:T(8,128)(2,1)} async-done(((bf16[64,512]{1,0:T(8,128)(2,1)}), bf16[4096,512]{1,0:T(8,128)(2,1)}) %all-gather.2.cloned.1.call-update) | async-done | bytes 4194320 | tf_op jit(solution)/shard_map/all_gather | solution.py:86
  220.1 3.2 fusion.8
  223.3 23.5 %all_to_all.67 = bf16[8,64,512]{2,1,0:T(8,128)(2,1)S(1)} all-to-all(bf16[8,64,512]{2,1,0:T(8,128)(2,1)S(1)} %broadcast_in_dim.36), channel_id=1, replica_groups=mesh['row'=16,'col'=4,'depth'=8] {'depth'}, dimensions={0} | all-to-all | bytes 1048576 | tf_op jit(solution)/shard_map/all_to_all | solution.py:16
  246.9 0.8 fusion
  247.8 19.7 %all_to_all.68 = bf16[8,64,512]{2,1,0:T(8,128)(2,1)S(1)} all-to-all(bf16[8,64,512]{2,1,0:T(8,128)(2,1)S(1)} %broadcast_in_dim.37), channel_id=1, replica_groups=mesh['row'=16,'col'=4,'depth'=8] {'depth'}, dimensions={0} | all-to-all | bytes 1048576 | tf_op jit(solution)/shard_map/all_to_all | solution.py:16
  267.6 0.8 fusion.1
  268.5 18.5 %all_to_all.69 = bf16[8,64,512]{2,1,0:T(8,128)(2,1)S(1)} all-to-all(bf16[8,64,512]{2,1,0:T(8,128)(2,1)S(1)} %broadcast_in_dim.38), channel_id=1, replica_groups=mesh['row'=16,'col'=4,'depth'=8] {'depth'}, dimensions={0} | all-to-all | bytes 1048576 | tf_op jit(solution)/shard_map/all_to_all | solution.py:16
  287.0 0.8 fusion.2
  287.9 17.6 %all_to_all.70 = bf16[8,64,512]{2,1,0:T(8,128)(2,1)S(1)} all-to-all(bf16[8,64,512]{2,1,0:T(8,128)(2,1)S(1)} %broadcast_in_dim.39), channel_id=1, replica_groups=mesh['row'=16,'col'=4,'depth'=8] {'depth'}, dimensions={0} | all-to-all | bytes 1048576 | tf_op jit(solution)/shard_map/all_to_all | solution.py:16
  305.6 0.8 fusion.3
  306.5 17.6 %all_to_all.71 = bf16[8,64,512]{2,1,0:T(8,128)(2,1)S(1)} all-to-all(bf16[8,64,512]{2,1,0:T(8,128)(2,1)S(1)} %broadcast_in_dim.40), channel_id=1, replica_groups=mesh['row'=16,'col'=4,'depth'=8] {'depth'}, dimensions={0} | all-to-all | bytes 1048576 | tf_op jit(solution)/shard_map/all_to_all | solution.py:16
  324.2 0.8 fusion.4
  325.0 0.8 broadcast_in_dim.41
  325.8 4.9 %all-to-all-start.9 = ((bf16[8,64,512]{2,1,0:T(8,128)(2,1)}), bf16[8,64,512]{2,1,0:T(8,128)(2,1)S(1)}, u32[]{:S(2)}, u32[]{:S(2)}) async-start(bf16[8,64,512]{2,1,0:T(8,128)(2,1)} %broadcast_in_dim.41), calls=%async_computation.9 | async-start | bytes 1048576 | tf_op jit(solution)/shard_map/all_to_all | solution.py:16
  330.7 13.0 %all-to-all-done.9 = bf16[8,64,512]{2,1,0:T(8,128)(2,1)S(1)} async-done(((bf16[8,64,512]{2,1,0:T(8,128)(2,1)}), bf16[8,64,512]{2,1,0:T(8,128)(2,1)S(1)}, u32[]{:S(2)}, u32[]{:S(2)}) %all-to-all-start.9) | async-done | bytes 524320 | tf_op jit(solution)/shard_map/all_to_all | solution.py:16
  343.7 3.7 %fusion.7 = f32[64,512]{1,0:T(8,128)} fusion(bf16[64,4096]{1,0:T(8,128)(2,1)S(1)} %bitcast.88, bf16[4096,512]{1,0:T(8,128)(2,1)} %all-gather.2.cloned.1.call-done, bf16[64,512]{1,0:T(8,128)(2,1)S(1)} %fusion.4, bf16[64,512]{1,0:T(8,128)(2,1)S(1)} %fusion.3, bf16[64,512]{1,0:T(8,128)(2,1)S(1)} %fusion.2, bf16[64,512]{1,0:T(8,128)(2,1)S(1)} %fusion.1, ...), kind=kOutput, calls=%fused_computation.19 | convolution fusion | flops 268992512 | bytes 5308420 | tf_op jit(solution)/shard_map/dot_general | solution.py:97
  (24 shorter events, 0.5 us)
Async XLA Ops:
  6.5 50.7 %copy-start.3 = (bf16[1,64,4096]{2,1,0:T(8,128)(2,1)S(1)}, bf16[1,64,4096]{2,1,0:T(8,128)(2,1)}, u32[]{:S(2)}) copy-start(bf16[1,64,4096]{2,1,0:T(8,128)(2,1)} %param.6) | copy-start | bytes 1572868
  6.5 50.7 %copy-start.2 = (bf16[1,64,4096]{2,1,0:T(8,128)(2,1)S(1)}, bf16[1,64,4096]{2,1,0:T(8,128)(2,1)}, u32[]{:S(2)}) copy-start(bf16[1,64,4096]{2,1,0:T(8,128)(2,1)} %param.5) | copy-start | bytes 1572868
  9.9 23.4 %all-to-all-start = ((bf16[64,1,2,64]{3,2,1,0:T(2,128)(2,1)}), bf16[64,1,2,64]{3,2,1,0:T(2,128)(2,1)S(1)}, u32[]{:S(2)}, u32[]{:S(2)}) async-start(bf16[64,1,2,64]{3,2,1,0:T(2,128)(2,1)} %broadcast_in_dim.34), calls=%async_computation | async-start | bytes 65536 | tf_op jit(solution)/shard_map/all_to_all | solution.py:16
  23.7 196.4 %all-gather.2.cloned.1.call-start = ((), (), s32[]{:S(2)}) async-start(), calls=%async_computation.10 | async-start | bytes 4259840 | tf_op jit(solution)/shard_map/all_gather | solution.py:86
  109.1 111.0 %copy-start.1 = (bf16[64,4096]{1,0:T(8,128)(2,1)S(1)}, bf16[64,4096]{1,0:T(8,128)(2,1)}, u32[]{:S(2)}) copy-start(bf16[64,4096]{1,0:T(8,128)(2,1)} %param.9) | copy-start | bytes 1572868
  220.1 26.8 %copy-start = (bf16[4096,512]{1,0:T(8,128)(2,1)S(1)}, bf16[4096,512]{1,0:T(8,128)(2,1)}, u32[]{:S(2)}) copy-start(bf16[4096,512]{1,0:T(8,128)(2,1)} %all-gather.2.cloned.1.call-done) | copy-start | bytes 12582916
  325.8 17.8 %all-to-all-start.9 = ((bf16[8,64,512]{2,1,0:T(8,128)(2,1)}), bf16[8,64,512]{2,1,0:T(8,128)(2,1)S(1)}, u32[]{:S(2)}, u32[]{:S(2)}) async-start(bf16[8,64,512]{2,1,0:T(8,128)(2,1)} %broadcast_in_dim.41), calls=%async_computation.9 | async-start | bytes 1048576 | tf_op jit(solution)/shard_map/all_to_all | solution.py:16
Sparse Core Ops, SparseCore 0:
  141.8 78.2 all-gather.1
where the time goes:
time: 355 us; the launch traced here: 354 us
  blocking collectives  184 us (52%)
  waiting for transfers between devices  98 us (28%)
  local copies, waits for them, and re-layouts  18.7 us (5%)
  starting transfers between devices  18.7 us (5%)
  between operations  14.4 us (4%)
  matrix products  11.2 us (3%)
  other arithmetic  9.01 us (3%)
    all_to_all x6, blocking collectives, from_everyone(): return lax.all_to_all(copies, axis, split_axis=0, concat_axis=0, tiled=True)  120 us
    all_gather x1, waiting for transfers between devices, per_device(): lax.all_gather(operator_piece, ('row', 'col'), axis=0, tiled=True)  78.4 us
    all_to_all x1, blocking collectives, per_device(): lax.all_to_all(local_sum, ('row', 'col'), split_axis=1, concat_axis=0, ti...  33.6 us
    all_to_all x1, blocking collectives, sum_at_owner(): lax.all_to_all(parts, axis, split_axis=0, concat_axis=0, tiled=True)  30.6 us
    all_to_all x2, waiting for transfers between devices, from_everyone(): return lax.all_to_all(copies, axis, split_axis=0, concat_axis=0, tiled=True)  19.6 us
    all_to_all x2, starting transfers between devices, from_everyone(): return lax.all_to_all(copies, axis, split_axis=0, concat_axis=0, tiled=True)  18.6 us
    dot_general x6, matrix products, per_device(): jnp.dot(piece, matching, preferred_element_type=jnp.float32)  7.87 us
  transfers between devices with their start and end apart: 3, of which 3 were waited for; matrix products, arithmetic and copies ran while one was open for 1% of the time, Pallas kernels for 0%

commit v1 on v0

v1 whole, which is shorter than its diff:
```python
import functools
import math

import jax
import jax.numpy as jnp
from jax import lax
from jax.experimental import pallas as pl
from jax.experimental.pallas import tpu as pltpu
from jax.sharding import Mesh, PartitionSpec as P

TERMS = 8
LATTICE = 0.25
CORES = 2


def exchange(pieces, axes):
    return lax.all_to_all(pieces, axes, split_axis=0, concat_axis=0, tiled=True)


def from_everyone(shard, axes):
    count = math.prod(lax.axis_size(axis) for axis in axes)
    return exchange(jnp.broadcast_to(shard, (count, *shard.shape)), axes)


def term_kernel(order, parts_ref, weight_ref, accum_ref, term_ref, total_ref, product):
    step = pl.program_id(0)
    span = parts_ref.shape[0]
    layers, lines = weight_ref.shape[1:3]
    rows = lines // span

    @pl.when(step == 0)
    def _():
        product[...] = jnp.zeros_like(product)

    for first in range(0, layers, 2):
        total = None
        for pair in range(0, span, 2):
            left = jnp.concatenate([parts_ref[x] for x in (pair, pair + 1)], axis=1)
            right = jnp.concatenate(
                [
                    jnp.concatenate(
                        [
                            weight_ref[side, layer, x * rows : (x + 1) * rows, :]
                            for x in (pair, pair + 1)
                            for side in range(CORES)
                        ],
                        axis=0,
                    )
                    for layer in (first, first + 1)
                ],
                axis=1,
            )
            part = jnp.dot(left, right, preferred_element_type=jnp.float32)
            total = part if total is None else total + part
        width = total.shape[1]
        at = first // 2 * width
        product[:, at : at + width] += total

    @pl.when(step == pl.num_programs(0) - 1)
    def _():
        term = (product[...] / order).astype(jnp.bfloat16)
        term_ref[...] = term
        total_ref[...] = accum_ref[...] + term.astype(jnp.float32)


def next_term(order, parts, weight, accum):
    groups, cores, layers, lines, twice = weight.shape
    span, count, width = parts.shape
    whole = pl.BlockSpec((count, width), lambda step: (0, 0))
    return pl.pallas_call(
        functools.partial(term_kernel, order),
        grid=(groups,),
        in_specs=[
            pl.BlockSpec((span, count, twice), lambda step: (0, 0, step)),
            pl.BlockSpec((None, cores, layers, lines, twice), lambda step: (step, 0, 0, 0, 0)),
            whole,
        ],
        out_specs=[whole, whole],
        out_shape=[
            jax.ShapeDtypeStruct((count, width), jnp.bfloat16),
            jax.ShapeDtypeStruct((count, width), jnp.float32),
        ],
        scratch_shapes=[pltpu.VMEM((count, width), jnp.float32)],
        compiler_params=pltpu.CompilerParams(dimension_semantics=("arbitrary",)),
        name="series_term",
    )(parts, weight, accum)


def per_device(intersection_re, intersection_im, weights, shells, rotation):
    groups = lax.axis_size("z")
    span = lax.axis_size("col")
    layers = lax.axis_size("depth")
    core = lax.axis_index("core")
    layer = lax.axis_index("depth")
    rows, width = intersection_re.shape[1:]
    block = width // groups
    position = lax.axis_index(("z", "core", "col"))

    eye = jnp.eye(rows, dtype=bool)

    def diagonal_of(values):
        square = lax.dynamic_slice_in_dim(values[0], position * rows, rows, 1)
        return jnp.sum(jnp.where(eye, square.astype(jnp.float32), 0.0), axis=0)

    piece = jnp.stack([diagonal_of(intersection_re), diagonal_of(intersection_im)]).astype(jnp.bfloat16)
    raw = jnp.stack([intersection_re[0], intersection_im[0]]).reshape(2, rows, groups, block)
    raw = jnp.moveaxis(raw, 2, 0)
    own_columns = from_everyone(piece, ("depth",))
    raw, own_columns = lax.optimization_barrier((raw, own_columns))
    raw = exchange(raw, "depth")
    diagonals = from_everyone(own_columns, ("z", "core", "col"))
    diagonals = diagonals.reshape(groups, -1, layers, 2, rows)
    diagonals = lax.dynamic_index_in_dim(diagonals, layer, 0, keepdims=False)
    diagonals = jnp.moveaxis(diagonals, 0, 2).reshape(layers, 2, block).astype(jnp.float32)
    diag_re = diagonals[:, 0]
    diag_im = diagonals[:, 1]
    vectors = shells.astype(jnp.float32) * LATTICE
    phase = jnp.arctan2(diag_im, diag_re)
    centre = -jnp.sum((weights[:, None] * vectors)[:, :, None] * phase[:, None, :], axis=0)
    spread = phase + jnp.sum(vectors[:, :, None] * centre[None], axis=1)
    ratio = spread / (diag_re * diag_re + diag_im * diag_im)
    scale_re = weights[:, None] * (diag_re + ratio * diag_im)
    scale_im = weights[:, None] * (diag_im - ratio * diag_re)

    raw = raw.astype(jnp.float32)
    grad = jnp.sum(raw[:, 0] * scale_re[:, None, :] + raw[:, 1] * scale_im[:, None, :], axis=0)

    direct = jnp.moveaxis(grad.reshape(rows, CORES, span, rows), 2, 0).reshape(span, rows, CORES * rows)
    direct = exchange(direct, "col").reshape(span * rows, CORES * rows)
    sides = grad.reshape(rows, CORES, span * rows)
    mirror = []
    for crossed in range(CORES):
        pairs = [
            ((z * CORES + c) * layers + y, (y * CORES + (c ^ crossed)) * layers + z)
            for z in range(groups)
            for c in range(CORES)
            for y in range(layers)
        ]
        half = lax.dynamic_index_in_dim(sides, core ^ crossed, 1, keepdims=False)
        mirror.append(lax.ppermute(half, ("z", "core", "depth"), pairs))
    lower = jnp.where(core == 0, mirror[0], mirror[1])
    upper = jnp.where(core == 0, mirror[1], mirror[0])
    mirrored = jnp.concatenate([lower, upper], axis=0).T
    factor = 1.25 / math.sqrt(weights.shape[0])
    operator = ((direct - mirrored) * factor).astype(jnp.bfloat16)
    operator = from_everyone(operator, ("depth",))
    operator = lax.all_gather(operator, ("z", "core"), axis=0, tiled=False)
    operator = operator.reshape(groups, CORES, layers, span * rows, CORES * rows)

    share = rows // layers
    own_rows = lax.dynamic_slice_in_dim(rotation, layer * share, share, 0)
    term = from_everyone(own_rows, ("col",)).reshape(span * share, groups * CORES, span, rows)
    parts = jnp.moveaxis(term, 2, 0).reshape(span, span * share, -1)
    accum = lax.dynamic_index_in_dim(parts, lax.axis_index("col"), 0, keepdims=False).astype(jnp.float32)
    for order in range(1, TERMS):
        term, accum = next_term(order, parts, operator, accum)
        if order + 1 < TERMS:
            parts = from_everyone(term, ("col",))

    out = jnp.moveaxis(accum.reshape(span, share, layers, CORES * rows), 2, 1)
    out = exchange(out.reshape(span * layers, share, CORES * rows), ("col", "depth"))
    out = out.reshape(span, layers, share, CORES, rows)
    return jnp.transpose(out, (1, 2, 3, 0, 4)).reshape(rows, block)


def solution(mesh):
    row, col, depth = mesh.devices.shape
    finer = Mesh(mesh.devices.reshape(row // CORES, CORES, col, depth), ("z", "core", "col", "depth"))
    lines = ("z", "core", "col")
    return jax.shard_map(
        per_device,
        mesh=finer,
        in_specs=(P("depth", lines, None), P("depth", lines, None), P(), P(), P(lines, None)),
        out_specs=P(lines, "depth"),
        check_vma=False,
    )
```

time: 355 us -> 322 us (0.907)
  blocking collectives: 184 us -> 104 us
  Pallas kernels: 0 us -> 52.2 us
  starting transfers between devices: 18.7 us -> 39.6 us
  matrix products: 11.2 us -> 0 us
  local copies, waits for them, and re-layouts: 18.7 us -> 13.3 us
  other arithmetic: 9.01 us -> 3.78 us
  waiting for transfers between devices: 98 us -> 93.6 us
    all_to_all x8, blocking collectives: 184 us -> 104 us  [exchange(): return lax.all_to_all(pieces, axes, split_axis=0, concat_axis=0, tiled=True)]
    pallas_call x0 -> x7, Pallas kernels: none -> 52.2 us  [next_term(): pl.pallas_call(functools.partial(term_kernel, order), grid=(groups,), in_...]
    all_gather x1, waiting for transfers between devices: 78.4 us -> 40.7 us  [per_device(): operator = lax.all_gather(operator, ('z', 'core'), axis=0, tiled=False)]
    all_to_all x2 -> x5, waiting for transfers between devices: 19.6 us -> 48.5 us  [exchange(): return lax.all_to_all(pieces, axes, split_axis=0, concat_axis=0, tiled=True)]
    all_to_all x2 -> x5, starting transfers between devices: 18.6 us -> 33 us  [exchange(): return lax.all_to_all(pieces, axes, split_axis=0, concat_axis=0, tiled=True)]
    dot_general x8 -> x0, matrix products: 11.2 us -> none  [the longest x6 7.87 us: per_device(): jnp.dot(piece, matching, preferred_element_type=jnp.float32)]
    all_to_all x4 -> x0, local copies, waits for them, and re-layouts: 7.09 us -> none  [per_device(): lax.all_to_all(local_sum, ('row', 'col'), split_axis=1, concat_axis=0, ti...]
    ppermute x0 -> x2, starting transfers between devices: none -> 6.56 us  [per_device(): mirror.append(lax.ppermute(half, ('z', 'core', 'depth'), pairs))]
  transfers between devices with their start and end apart: 3 -> 8, of which waited for: 3 -> 8; matrix products, arithmetic and copies ran while one was open for 1% -> 2% of each run, Pallas kernels for 0% -> 0%
where the time goes in v1:
time: 322 us; the launch traced here: 320 us
  blocking collectives  104 us (32%)
  waiting for transfers between devices  93.6 us (29%)
  Pallas kernels  52.2 us (16%)
  starting transfers between devices  39.6 us (12%)
  between operations  13.8 us (4%)
  local copies, waits for them, and re-layouts  13.3 us (4%)
  other arithmetic  3.78 us (1%)
    all_to_all x8, blocking collectives, exchange(): return lax.all_to_all(pieces, axes, split_axis=0, concat_axis=0, tiled=True)  104 us
    pallas_call x7, Pallas kernels, next_term(): pl.pallas_call(functools.partial(term_kernel, order), grid=(groups,), in_...  52.2 us
    all_to_all x5, waiting for transfers between devices, exchange(): return lax.all_to_all(pieces, axes, split_axis=0, concat_axis=0, tiled=True)  48.5 us
    all_gather x1, waiting for transfers between devices, per_device(): operator = lax.all_gather(operator, ('z', 'core'), axis=0, tiled=False)  40.7 us
    all_to_all x5, starting transfers between devices, exchange(): return lax.all_to_all(pieces, axes, split_axis=0, concat_axis=0, tiled=True)  33 us
    ppermute x2, starting transfers between devices, per_device(): mirror.append(lax.ppermute(half, ('z', 'core', 'depth'), pairs))  6.56 us
    broadcast_in_dim x9, local copies, waits for them, and re-layouts, from_everyone(): return exchange(jnp.broadcast_to(shard, (count, *shard.shape)), axes)  6.55 us
  transfers between devices with their start and end apart: 8, of which 8 were waited for; matrix products, arithmetic and copies ran while one was open for 2% of the time, Pallas kernels for 0%

profile of v1, /device:TPU:8, one launch (start us, length us, event | category | flops | bytes accessed | tf_op | source)
XLA Modules:
  0.0 320.0 jit_solution(15005794101374848829)
XLA Ops:
  6.5 0.9 fusion.7
  7.4 0.6 broadcast_in_dim.46
  8.0 9.0 %all-to-all-start.1 = ((bf16[8,2,64]{2,1,0:T(2,128)(2,1)}), bf16[8,2,64]{2,1,0:T(2,128)(2,1)S(1)}, u32[]{:S(2)}, u32[]{:S(2)}) async-start(bf16[8,2,64]{2,1,0:T(2,128)(2,1)} %broadcast_in_dim.46), calls=%async_computation.1 | async-start | bytes 8192 | tf_op jit(solution)/shard_map/all_to_all | solution.py:17
  17.0 1.3 pad_maximum_fusion
  18.3 0.4 copy.57
  18.8 4.4 %all-to-all-done.1 = bf16[8,2,64]{2,1,0:T(2,128)(2,1)S(1)} async-done(((bf16[8,2,64]{2,1,0:T(2,128)(2,1)}), bf16[8,2,64]{2,1,0:T(2,128)(2,1)S(1)}, u32[]{:S(2)}, u32[]{:S(2)}) %all-to-all-start.1) | async-done | bytes 2080 | tf_op jit(solution)/shard_map/all_to_all | solution.py:17
  23.3 0.8 reshape.89
  24.1 12.3 %all-to-all-start.3 = ((bf16[64,2,512]{2,1,0:T(2,128)(2,1)}), bf16[64,2,512]{2,1,0:T(2,128)(2,1)S(1)}, u32[]{:S(2)}, u32[]{:S(2)}) async-start(bf16[64,2,512]{2,1,0:T(2,128)(2,1)} %reshape.89), calls=%async_computation.3 | async-start | bytes 262144 | tf_op jit(solution)/shard_map/all_to_all | solution.py:17
  36.5 1.3 copy.42
  37.8 10.1 %all-to-all-done.3 = bf16[64,2,512]{2,1,0:T(2,128)(2,1)S(1)} async-done(((bf16[64,2,512]{2,1,0:T(2,128)(2,1)}), bf16[64,2,512]{2,1,0:T(2,128)(2,1)S(1)}, u32[]{:S(2)}, u32[]{:S(2)}) %all-to-all-start.3) | async-done | bytes 131104 | tf_op jit(solution)/shard_map/all_to_all | solution.py:17
  47.9 4.9 %all-to-all-start.2 = ((bf16[8,2,64,512]{3,2,1,0:T(8,128)(2,1)}), bf16[8,2,64,512]{3,2,1,0:T(8,128)(2,1)S(1)}, u32[]{:S(2)}, u32[]{:S(2)}) async-start(bf16[8,2,64,512]{3,2,1,0:T(8,128)(2,1)} %copy.42), calls=%async_computation.2 | async-start | bytes 2097152 | tf_op jit(solution)/shard_map/all_to_all | solution.py:17
  53.5 25.7 %all-to-all-done.2 = bf16[8,2,64,512]{3,2,1,0:T(8,128)(2,1)S(1)} async-done(((bf16[8,2,64,512]{3,2,1,0:T(8,128)(2,1)}), bf16[8,2,64,512]{3,2,1,0:T(8,128)(2,1)S(1)}, u32[]{:S(2)}, u32[]{:S(2)}) %all-to-all-start.2) | async-done | bytes 1048608 | tf_op jit(solution)/shard_map/all_to_all | solution.py:17
  80.0 4.6 %collective-permute-start = (f32[64,256]{1,0:T(8,128)S(1)}, f32[64,256]{1,0:T(8,128)S(1)}, u32[]{:S(2)}, u32[]{:S(2)}) collective-permute-start(f32[64,256]{1,0:T(8,128)S(1)} %bitcast.109), channel_id=1, source_target_pairs={{0,0},{1,64},{2,128},{3,192},{4,256},{5,320},{6,384},{7,448},{32,3... | collective-permute-start | bytes 196616 | tf_op jit(solution)/shard_map/ppermute | solution.py:140
  84.7 1.9 collective-permute-start.1
  86.9 0.8 reshape.74
  87.7 3.3 %all-to-all-start.4 = ((f32[4,64,128]{2,1,0:T(8,128)}), f32[4,64,128]{2,1,0:T(8,128)S(1)}, u32[]{:S(2)}, u32[]{:S(2)}) async-start(f32[4,64,128]{2,1,0:T(8,128)} %reshape.74), calls=%async_computation.4 | async-start | bytes 262144 | tf_op jit(solution)/shard_map/all_to_all | solution.py:17
  91.1 3.3 %collective-permute-done = f32[64,256]{1,0:T(8,128)S(1)} collective-permute-done((f32[64,256]{1,0:T(8,128)S(1)}, f32[64,256]{1,0:T(8,128)S(1)}, u32[]{:S(2)}, u32[]{:S(2)}) %collective-permute-start) | collective-permute-done | bytes 65568 | tf_op jit(solution)/shard_map/ppermute | solution.py:140
  94.4 1.0 collective-permute-done.1
  95.4 1.6 all-to-all-done.4
  97.4 26.3 %all_to_all.65 = bf16[8,256,128]{2,1,0:T(8,128)(2,1)} all-to-all(bf16[8,256,128]{2,1,0:T(8,128)(2,1)S(1)} %broadcast_in_dim.48), channel_id=1, replica_groups=mesh['z'=8,'core'=2,'col'=4,'depth'=8] {'depth'}, dimensions={0} | all-to-all | bytes 1048576 | tf_op jit(solution)/shard_map/all_to_all | solution.py:17
  123.7 0.7 broadcast_in_dim.44
  124.5 3.4 %all-to-all-start = ((bf16[4,8,4096]{2,1,0:T(8,128)(2,1)}), bf16[4,8,4096]{2,1,0:T(8,128)(2,1)S(1)}, u32[]{:S(2)}, u32[]{:S(2)}) async-start(bf16[4,8,4096]{2,1,0:T(8,128)(2,1)} %broadcast_in_dim.44), calls=%async_computation | async-start | bytes 524288 | tf_op jit(solution)/shard_map/all_to_all | solution.py:17
  127.9 6.6 %all-to-all-done = bf16[4,8,4096]{2,1,0:T(8,128)(2,1)S(1)} async-done(((bf16[4,8,4096]{2,1,0:T(8,128)(2,1)}), bf16[4,8,4096]{2,1,0:T(8,128)(2,1)S(1)}, u32[]{:S(2)}, u32[]{:S(2)}) %all-to-all-start) | async-done | bytes 262176 | tf_op jit(solution)/shard_map/all_to_all | solution.py:17
  134.5 0.5 reshape.69
  135.2 0.3 reshape.70.parts_ref
  135.5 0.7 bitcast_convert_fusion.accum_ref
  136.3 40.7 %all-gather.3.cloned.1.call-done = bf16[128,256,128]{2,1,0:T(8,128)(2,1)} async-done(((bf16[8,256,128]{2,1,0:T(8,128)(2,1)}), bf16[128,256,128]{2,1,0:T(8,128)(2,1)}) %all-gather.3.cloned.1.call-update) | async-done | bytes 8388624 | tf_op jit(solution)/shard_map/all_gather | solution.py:147
  177.0 7.5 %series_term.7 = (bf16[32,1024]{1,0:T(8,128)(2,1)}, f32[32,1024]{1,0:T(8,128)}) custom-call(bf16[4,32,1024]{2,1,0:T(8,128)(2,1)} %copy-done.1, bf16[8,2,8,256,128]{4,3,2,1,0:T(8,128)(2,1)} %bitcast.94, f32[32,1024]{1,0:T(8,128)} %bitcast_convert_fusion.accum_ref), custom_call_target="tpu_custom_call" | custom-call | tf_op jit(solution)/shard_map/series_term/pallas_call | solution.py:70
  184.5 0.9 broadcast_in_dim.49
  185.3 11.2 %all_to_all.66.parts_ref = bf16[4,32,1024]{2,1,0:T(8,128)(2,1)} all-to-all(bf16[4,32,1024]{2,1,0:T(8,128)(2,1)S(1)} %broadcast_in_dim.49), channel_id=1, replica_groups=mesh['z'=8,'core'=2,'col'=4,'depth'=8] {'col'}, dimensions={0} | all-to-all | bytes 524288 | tf_op jit(solution)/shard_map/all_to_all | solution.py:17
  196.5 7.4 %series_term.8 = (bf16[32,1024]{1,0:T(8,128)(2,1)}, f32[32,1024]{1,0:T(8,128)}) custom-call(bf16[4,32,1024]{2,1,0:T(8,128)(2,1)} %all_to_all.66.parts_ref, bf16[8,2,8,256,128]{4,3,2,1,0:T(8,128)(2,1)} %bitcast.95, f32[32,1024]{1,0:T(8,128)} %get-tuple-element.23.accum_ref), custom_call_target="tpu_custom_call" | custom-call | tf_op jit(solution)/shard_map/series_term/pallas_call | solution.py:70
  204.0 0.9 broadcast_in_dim.50
  204.9 9.7 %all_to_all.67.parts_ref = bf16[4,32,1024]{2,1,0:T(8,128)(2,1)} all-to-all(bf16[4,32,1024]{2,1,0:T(8,128)(2,1)S(1)} %broadcast_in_dim.50), channel_id=1, replica_groups=mesh['z'=8,'core'=2,'col'=4,'depth'=8] {'col'}, dimensions={0} | all-to-all | bytes 524288 | tf_op jit(solution)/shard_map/all_to_all | solution.py:17
  214.6 7.5 %series_term.9 = (bf16[32,1024]{1,0:T(8,128)(2,1)}, f32[32,1024]{1,0:T(8,128)}) custom-call(bf16[4,32,1024]{2,1,0:T(8,128)(2,1)} %all_to_all.67.parts_ref, bf16[8,2,8,256,128]{4,3,2,1,0:T(8,128)(2,1)} %bitcast.96, f32[32,1024]{1,0:T(8,128)} %get-tuple-element.25.accum_ref), custom_call_target="tpu_custom_call" | custom-call | tf_op jit(solution)/shard_map/series_term/pallas_call | solution.py:70
  222.1 0.9 broadcast_in_dim.51
  222.9 9.7 %all_to_all.68.parts_ref = bf16[4,32,1024]{2,1,0:T(8,128)(2,1)} all-to-all(bf16[4,32,1024]{2,1,0:T(8,128)(2,1)S(1)} %broadcast_in_dim.51), channel_id=1, replica_groups=mesh['z'=8,'core'=2,'col'=4,'depth'=8] {'col'}, dimensions={0} | all-to-all | bytes 524288 | tf_op jit(solution)/shard_map/all_to_all | solution.py:17
  232.7 7.4 %series_term.10 = (bf16[32,1024]{1,0:T(8,128)(2,1)}, f32[32,1024]{1,0:T(8,128)}) custom-call(bf16[4,32,1024]{2,1,0:T(8,128)(2,1)} %all_to_all.68.parts_ref, bf16[8,2,8,256,128]{4,3,2,1,0:T(8,128)(2,1)} %bitcast.97, f32[32,1024]{1,0:T(8,128)} %get-tuple-element.27.accum_ref), custom_call_target="tpu_custom_call" | custom-call | tf_op jit(solution)/shard_map/series_term/pallas_call | solution.py:70
  240.1 0.9 broadcast_in_dim.52
  241.0 9.7 %all_to_all.69.parts_ref = bf16[4,32,1024]{2,1,0:T(8,128)(2,1)} all-to-all(bf16[4,32,1024]{2,1,0:T(8,128)(2,1)S(1)} %broadcast_in_dim.52), channel_id=1, replica_groups=mesh['z'=8,'core'=2,'col'=4,'depth'=8] {'col'}, dimensions={0} | all-to-all | bytes 524288 | tf_op jit(solution)/shard_map/all_to_all | solution.py:17
  250.7 7.5 %series_term.11 = (bf16[32,1024]{1,0:T(8,128)(2,1)}, f32[32,1024]{1,0:T(8,128)}) custom-call(bf16[4,32,1024]{2,1,0:T(8,128)(2,1)} %all_to_all.69.parts_ref, bf16[8,2,8,256,128]{4,3,2,1,0:T(8,128)(2,1)} %bitcast.98, f32[32,1024]{1,0:T(8,128)} %get-tuple-element.29.accum_ref), custom_call_target="tpu_custom_call" | custom-call | tf_op jit(solution)/shard_map/series_term/pallas_call | solution.py:70
  258.2 0.9 broadcast_in_dim.53
  259.0 9.7 %all_to_all.70.parts_ref = bf16[4,32,1024]{2,1,0:T(8,128)(2,1)} all-to-all(bf16[4,32,1024]{2,1,0:T(8,128)(2,1)S(1)} %broadcast_in_dim.53), channel_id=1, replica_groups=mesh['z'=8,'core'=2,'col'=4,'depth'=8] {'col'}, dimensions={0} | all-to-all | bytes 524288 | tf_op jit(solution)/shard_map/all_to_all | solution.py:17
  268.8 7.4 %series_term.12 = (bf16[32,1024]{1,0:T(8,128)(2,1)}, f32[32,1024]{1,0:T(8,128)}) custom-call(bf16[4,32,1024]{2,1,0:T(8,128)(2,1)} %all_to_all.70.parts_ref, bf16[8,2,8,256,128]{4,3,2,1,0:T(8,128)(2,1)} %bitcast.99, f32[32,1024]{1,0:T(8,128)} %get-tuple-element.31.accum_ref), custom_call_target="tpu_custom_call" | custom-call | tf_op jit(solution)/shard_map/series_term/pallas_call | solution.py:70
  276.2 0.9 broadcast_in_dim.54
  277.1 9.7 %all_to_all.71.parts_ref = bf16[4,32,1024]{2,1,0:T(8,128)(2,1)} all-to-all(bf16[4,32,1024]{2,1,0:T(8,128)(2,1)S(1)} %broadcast_in_dim.54), channel_id=1, replica_groups=mesh['z'=8,'core'=2,'col'=4,'depth'=8] {'col'}, dimensions={0} | all-to-all | bytes 524288 | tf_op jit(solution)/shard_map/all_to_all | solution.py:17
  286.8 7.5 %series_term.13 = (bf16[32,1024]{1,0:T(8,128)(2,1)}, f32[32,1024]{1,0:T(8,128)}) custom-call(bf16[4,32,1024]{2,1,0:T(8,128)(2,1)} %all_to_all.71.parts_ref, bf16[8,2,8,256,128]{4,3,2,1,0:T(8,128)(2,1)} %bitcast.100, f32[32,1024]{1,0:T(8,128)} %get-tuple-element.33.accum_ref), custom_call_target="tpu_custom_call" | custom-call | tf_op jit(solution)/shard_map/series_term/pallas_call | solution.py:70
  294.3 17.7 %all_to_all.72 = f32[32,8,128]{2,1,0:T(8,128)S(1)} all-to-all(f32[32,8,128]{2,1,0:T(8,128)} %bitcast.108), channel_id=1, replica_groups=mesh['z'=8,'core'=2,'col'=4,'depth'=8] {'col','depth'}, dimensions={0} | all-to-all | bytes 262144 | tf_op jit(solution)/shard_map/all_to_all | solution.py:17
  312.4 0.8 reshape.81
  (42 shorter events, 2.6 us)
Async XLA Ops:
  6.5 117.2 %copy-start = (bf16[64,4096]{1,0:T(8,128)(2,1)S(1)}, bf16[64,4096]{1,0:T(8,128)(2,1)}, u32[]{:S(2)}) copy-start(bf16[64,4096]{1,0:T(8,128)(2,1)} %param.9) | copy-start | bytes 1572868
  8.0 15.2 %all-to-all-start.1 = ((bf16[8,2,64]{2,1,0:T(2,128)(2,1)}), bf16[8,2,64]{2,1,0:T(2,128)(2,1)S(1)}, u32[]{:S(2)}, u32[]{:S(2)}) async-start(bf16[8,2,64]{2,1,0:T(2,128)(2,1)} %broadcast_in_dim.46), calls=%async_computation.1 | async-start | bytes 8192 | tf_op jit(solution)/shard_map/all_to_all | solution.py:17
  24.1 23.7 %all-to-all-start.3 = ((bf16[64,2,512]{2,1,0:T(2,128)(2,1)}), bf16[64,2,512]{2,1,0:T(2,128)(2,1)S(1)}, u32[]{:S(2)}, u32[]{:S(2)}) async-start(bf16[64,2,512]{2,1,0:T(2,128)(2,1)} %reshape.89), calls=%async_computation.3 | async-start | bytes 262144 | tf_op jit(solution)/shard_map/all_to_all | solution.py:17
  36.5 16.3 %copy-start.3 = (f32[8]{0:T(128)S(1)}, f32[8]{0:T(128)}, u32[]{:S(2)}) copy-start(f32[8]{0:T(128)} %param.7) | copy-start | bytes 100
  36.5 16.3 %copy-start.2 = (s32[8,3]{0,1:T(4,128)S(1)}, s32[8,3]{0,1:T(4,128)}, u32[]{:S(2)}) copy-start(s32[8,3]{0,1:T(4,128)} %param.8) | copy-start | bytes 292
  47.9 31.3 %all-to-all-start.2 = ((bf16[8,2,64,512]{3,2,1,0:T(8,128)(2,1)}), bf16[8,2,64,512]{3,2,1,0:T(8,128)(2,1)S(1)}, u32[]{:S(2)}, u32[]{:S(2)}) async-start(bf16[8,2,64,512]{3,2,1,0:T(8,128)(2,1)} %copy.42), calls=%async_computation.2 | async-start | bytes 2097152 | tf_op jit(solution)/shard_map/all_to_all | solution.py:17
  80.0 14.4 %collective-permute-start = (f32[64,256]{1,0:T(8,128)S(1)}, f32[64,256]{1,0:T(8,128)S(1)}, u32[]{:S(2)}, u32[]{:S(2)}) collective-permute-start(f32[64,256]{1,0:T(8,128)S(1)} %bitcast.109), channel_id=1, source_target_pairs={{0,0},{1,64},{2,128},{3,192},{4,256},{5,320},{6,384},{7,448},{32,3... | collective-permute-start | bytes 196616 | tf_op jit(solution)/shard_map/ppermute | solution.py:140
  84.7 10.8 %collective-permute-start.1 = (f32[64,256]{1,0:T(8,128)S(1)}, f32[64,256]{1,0:T(8,128)S(1)}, u32[]{:S(2)}, u32[]{:S(2)}) collective-permute-start(f32[64,256]{1,0:T(8,128)S(1)} %bitcast.110), channel_id=1, source_target_pairs={{0,32},{1,96},{2,160},{3,224},{4,288},{5,352},{6,416},{7,480},{32,... | collective-permute-start | bytes 196616 | tf_op jit(solution)/shard_map/ppermute | solution.py:140
  87.7 9.3 %all-to-all-start.4 = ((f32[4,64,128]{2,1,0:T(8,128)}), f32[4,64,128]{2,1,0:T(8,128)S(1)}, u32[]{:S(2)}, u32[]{:S(2)}) async-start(f32[4,64,128]{2,1,0:T(8,128)} %reshape.74), calls=%async_computation.4 | async-start | bytes 262144 | tf_op jit(solution)/shard_map/all_to_all | solution.py:17
  91.1 85.9 %all-gather.3.cloned.1.call-start = ((), (), s32[]{:S(2)}) async-start(), calls=%async_computation.13 | async-start | bytes 8912896 | tf_op jit(solution)/shard_map/all_gather | solution.py:147
  124.5 10.1 %all-to-all-start = ((bf16[4,8,4096]{2,1,0:T(8,128)(2,1)}), bf16[4,8,4096]{2,1,0:T(8,128)(2,1)S(1)}, u32[]{:S(2)}, u32[]{:S(2)}) async-start(bf16[4,8,4096]{2,1,0:T(8,128)(2,1)} %broadcast_in_dim.44), calls=%async_computation | async-start | bytes 524288 | tf_op jit(solution)/shard_map/all_to_all | solution.py:17
  135.5 41.5 %copy-start.1 = (bf16[4,32,1024]{2,1,0:T(8,128)(2,1)}, bf16[4,32,1024]{2,1,0:T(8,128)(2,1)S(1)}, u32[]{:S(2)}) copy-start(bf16[4,32,1024]{2,1,0:T(8,128)(2,1)S(1)} %reshape.70.parts_ref) | copy-start | bytes 786436
Sparse Core Ops, SparseCore 0:
  123.8 53.1 all-gather.2
